TPU v7x, 32 devices: a whole 2x2x4 slice. The times are simulated.
32 devices in a mesh: row: 8 (over z, y), col: 4 (over x, core).
Axes of the slice: x: 2, y: 2, z: 4, core: 2. Of those that a mesh axis runs over, the one named last changes fastest.
Arguments:
- right_side: float32 [8, 4, 8, 128], P('row', 'col'), may hold values from -6 to 6
- block_values: bfloat16 [8, 4, 8, 4, 128, 128], P('row', 'col'), may hold values from -0.25 to 0.25
- block_columns: int32 [8, 4, 8, 4], P('row', 'col'), may hold values from 0 to 71
- live_slots: int32 [8, 4, 8], P('row', 'col'), may hold values from 1 to 4
- row_scale: float32 [8, 4, 8, 128], P('row', 'col'), may hold values from 1 to 4
Outputs:
- solution_field: float32 [8, 4, 8, 128], P('row', 'col')
- hessenberg: float32 [5, 4], replicated
Inputs may be any that keep to these rules, and one draw needn't show every extreme that they name: `block_columns`: an entry q names block q % 8 of the device at grid offset (q // 24 - 1, (q // 8) % 3 - 1); blocks outside the grid are zero. Only the first live_slots slots of a block row are used.
All inputs are finite; a program needn't handle non-finite values.
Results may differ from a plain program's by a relative error of at most 0.0012.
Values may be sent and summed in bfloat16 or wider, within the bound.
A program may use at most 64 MiB of HBM per device.

v0:
```python
import jax
import jax.numpy as jnp
from jax import lax
from jax.sharding import PartitionSpec as P

ITERS = 4


def padded(x, sides, width):
    for axis, dim in sides:
        count, length = (lax.axis_size(axis), x.shape[dim])
        up = [(i, (i + 1) % count) for i in range(count - 1)]
        down = [(j, i) for i, j in up]
        last = lax.slice_in_dim(x, length - width, length, axis=dim)
        first = lax.slice_in_dim(x, 0, width, axis=dim)
        before = lax.ppermute(last, axis, up)
        after = lax.ppermute(first, axis, down)
        x = jnp.concatenate([before, x, after], axis=dim)
    return x


def neighbourhood(rounded):
    return padded(rounded, (("row", 0), ("col", 1)), 1)


def global_sum(dot_terms, square_term):
    partial_dots, partial_square = lax.psum((dot_terms, square_term), "col")
    return lax.psum((partial_dots, partial_square), "row")


def least_squares(hessenberg, initial_norm):
    gram = jnp.dot(hessenberg.T, hessenberg, precision=lax.Precision.HIGHEST)
    target = initial_norm * hessenberg[0, :]
    factor = jnp.linalg.cholesky(gram)
    steps_count = gram.shape[0]
    forward = []
    for ordinal in range(steps_count):
        accum = target[ordinal]
        for other in range(ordinal):
            accum = accum - factor[ordinal, other] * forward[other]
        forward.append(accum / factor[ordinal, ordinal])
    backward = [None] * steps_count
    for ordinal in reversed(range(steps_count)):
        accum = forward[ordinal]
        for other in range(ordinal + 1, steps_count):
            accum = accum - factor[other, ordinal] * backward[other]
        backward[ordinal] = accum / factor[ordinal, ordinal]
    return backward


def on_device(right_side, block_values, block_columns, live_slots, row_scale):
    blocks_dev = right_side.shape[2]
    block_size = right_side.shape[3]
    slot_count = block_values.shape[3]
    values = block_values.reshape(blocks_dev, slot_count, block_size, block_size)
    slot_index = block_columns.reshape(-1)
    live_mask = (
        jnp.arange(slot_count, dtype=jnp.int32)[None, :] < live_slots.reshape(blocks_dev, 1)
    ).astype(jnp.bfloat16)[..., None]

    def operate(field):
        rounded = field.astype(jnp.bfloat16)
        beside_all = neighbourhood(rounded).reshape(9 * blocks_dev, block_size)
        picked = beside_all[slot_index].reshape(blocks_dev, slot_count, block_size) * live_mask
        product = jnp.einsum("nsij,nsj->ni", values, picked, preferred_element_type=jnp.float32)
        return row_scale * field + product.reshape(field.shape)

    first_image = operate(right_side)
    local_dots = jnp.stack([jnp.sum(right_side * right_side), jnp.sum(right_side * first_image)])
    summed_dots, image_dot = global_sum(local_dots, jnp.sum(first_image * first_image))
    self_dot = summed_dots[0]
    initial_norm = jnp.sqrt(self_dot)
    basis = [right_side / initial_norm]
    residue = first_image / initial_norm
    projections = jnp.stack([summed_dots[1] / self_dot])
    norm_square = image_dot / self_dot
    columns = []
    for iteration in range(ITERS):
        if iteration > 0:
            residue = operate(basis[-1])
            local_proj = jnp.stack([jnp.sum(vector * residue) for vector in basis])
            projections, norm_square = global_sum(local_proj, jnp.sum(residue * residue))
        height = jnp.sqrt(norm_square - jnp.sum(projections * projections))
        columns.append(
            jnp.concatenate(
                [projections, height[None], jnp.zeros((ITERS - iteration - 1,), jnp.float32)]
            )
        )
        if iteration + 1 < ITERS:
            for ordinal in range(len(basis)):
                residue = residue - projections[ordinal] * basis[ordinal]
            basis.append(residue / height)
    hessenberg = jnp.stack(columns, axis=1)
    weights = least_squares(hessenberg, initial_norm)
    solution_field = weights[0] * basis[0]
    for ordinal in range(1, ITERS):
        solution_field = solution_field + weights[ordinal] * basis[ordinal]
    return (solution_field, hessenberg)


def solution(mesh):
    return jax.shard_map(
        on_device,
        mesh=mesh,
        in_specs=(
            P("row", "col", None, None),
            P("row", "col", None, None, None, None),
            P("row", "col", None, None),
            P("row", "col", None),
            P("row", "col", None, None),
        ),
        out_specs=(P("row", "col", None, None), P()),
        check_vma=False,
    )
```

profile of v0, /device:TPU:0, one launch (start us, length us, event | category | flops | bytes accessed | tf_op | source)
XLA Modules:
  0.0 215.7 jit_solution(13172974615176893800)
XLA Ops:
  0.7 0.8 convert_element_type.19
  1.4 1.4 collective-permute-start.1
  2.9 5.5 %collective-permute-start = (bf16[1,1,8,128]{3,2,1,0:T(8,128)(2,1)S(1)}, bf16[1,1,8,128]{3,2,1,0:T(8,128)(2,1)S(1)}, u32[]{:S(2)}, u32[]{:S(2)}) collective-permute-start(bf16[1,1,8,128]{3,2,1,0:T(8,128)(2,1)S(1)} %convert_element_type.19), channel_id=1, source_target_pairs={{0,4},{4,8},{8,12},{12,16},{16,20},{20,24},{24,28},{1,5},{5,9},{9,... | collective-permute-start | bytes 6152 | tf_op jit(solution)/shard_map/ppermute | solution.py:16
  8.7 1.0 collective-permute-done
  9.7 1.3 collective-permute-start.3
  11.0 3.0 %collective-permute-start.2 = (bf16[3,1,8,128]{3,2,1,0:T(8,128)(2,1)S(1)}, bf16[3,1,8,128]{3,2,1,0:T(8,128)(2,1)S(1)}, u32[]{:S(2)}, u32[]{:S(2)}) collective-permute-start(bf16[3,1,8,128]{3,2,1,0:T(8,128)(2,1)S(1)} %pad_maximum_fusion.4), channel_id=1, source_target_pairs={{0,1},{1,2},{2,3},{4,5},{5,6},{6,7},{8,9},{9,10},{10,11},{12,13},{... | collective-permute-start | bytes 18440 | tf_op jit(solution)/shard_map/ppermute | solution.py:16
  14.0 0.8 collective-permute-done.2
  14.8 0.6 gather_fusion
  15.5 0.4 fusion.6
  16.2 0.7 multiply_reduce_fusion.14
  16.9 1.4 pad_maximum_fusion.9
  18.3 8.2 %all-reduce.7 = (f32[]{:T(128)}, f32[2]{0:T(128)S(1)}) all-reduce(f32[]{:T(128)} %get-tuple-element.16, f32[2]{0:T(128)S(1)} %pad_maximum_fusion.9), channel_id=1, replica_groups=mesh['row'=8,'col'=4] {'col'}, use_global_device_ids=true, to_apply=%region_5.0 | all-reduce | flops 3 | bytes 24 | tf_op jit(solution)/shard_map/psum | solution.py:27
  26.5 23.0 %all-reduce.3 = (f32[]{:T(128)}, f32[2]{0:T(128)S(1)}) all-reduce(f32[]{:T(128)} %get-tuple-element.31, f32[2]{0:T(128)S(1)} %get-tuple-element.32), channel_id=1, replica_groups=mesh['row'=8,'col'=4] {'row'}, use_global_device_ids=true, to_apply=%region_6.0 | all-reduce | flops 3 | bytes 24 | tf_op jit(solution)/shard_map/psum | solution.py:28
  49.5 0.6 fusion.22
  53.6 1.3 collective-permute-start.5
  54.9 4.5 %collective-permute-start.4 = (bf16[1,1,8,128]{3,2,1,0:T(8,128)(2,1)S(1)}, bf16[1,1,8,128]{3,2,1,0:T(8,128)(2,1)S(1)}, u32[]{:S(2)}, u32[]{:S(2)}) collective-permute-start(bf16[1,1,8,128]{3,2,1,0:T(8,128)(2,1)S(1)} %get-tuple-element.39), channel_id=1, source_target_pairs={{0,4},{4,8},{8,12},{12,16},{16,20},{20,24},{24,28},{1,5},{5,9},{9,... | collective-permute-start | bytes 6152 | tf_op jit(solution)/shard_map/ppermute | solution.py:16
  59.5 1.3 collective-permute-done.4
  60.8 1.3 collective-permute-start.7
  62.1 3.0 %collective-permute-start.6 = (bf16[3,1,8,128]{3,2,1,0:T(8,128)(2,1)S(1)}, bf16[3,1,8,128]{3,2,1,0:T(8,128)(2,1)S(1)}, u32[]{:S(2)}, u32[]{:S(2)}) collective-permute-start(bf16[3,1,8,128]{3,2,1,0:T(8,128)(2,1)S(1)} %pad_maximum_fusion.5), channel_id=1, source_target_pairs={{0,1},{1,2},{2,3},{4,5},{5,6},{6,7},{8,9},{9,10},{10,11},{12,13},{... | collective-permute-start | bytes 18440 | tf_op jit(solution)/shard_map/ppermute | solution.py:16
  65.1 0.8 collective-permute-done.6
  65.9 0.6 gather_fusion.1
  66.6 0.4 fusion.4
  67.0 0.7 multiply_reduce_fusion.11
  67.7 1.3 pad_maximum_fusion.10
  69.0 8.1 %all-reduce.6 = (f32[]{:T(128)}, f32[2]{0:T(128)S(1)}) all-reduce(f32[]{:T(128)} %get-tuple-element.12, f32[2]{0:T(128)S(1)} %pad_maximum_fusion.10), channel_id=1, replica_groups=mesh['row'=8,'col'=4] {'col'}, use_global_device_ids=true, to_apply=%region_12.0 | all-reduce | flops 3 | bytes 24 | tf_op jit(solution)/shard_map/psum | solution.py:27
  77.1 20.1 %all-reduce.2 = (f32[]{:T(128)}, f32[2]{0:T(128)S(1)}) all-reduce(f32[]{:T(128)} %get-tuple-element.29, f32[2]{0:T(128)S(1)} %get-tuple-element.30), channel_id=1, replica_groups=mesh['row'=8,'col'=4] {'row'}, use_global_device_ids=true, to_apply=%region_13.0 | all-reduce | flops 3 | bytes 24 | tf_op jit(solution)/shard_map/psum | solution.py:28
  97.1 0.7 multiply_reduce_fusion.17
  97.8 0.6 fusion.21
  99.8 1.2 fusion.16
  101.0 1.3 collective-permute-start.9
  102.3 4.5 %collective-permute-start.8 = (bf16[1,1,8,128]{3,2,1,0:T(8,128)(2,1)S(1)}, bf16[1,1,8,128]{3,2,1,0:T(8,128)(2,1)S(1)}, u32[]{:S(2)}, u32[]{:S(2)}) collective-permute-start(bf16[1,1,8,128]{3,2,1,0:T(8,128)(2,1)S(1)} %get-tuple-element.36), channel_id=1, source_target_pairs={{0,4},{4,8},{8,12},{12,16},{16,20},{20,24},{24,28},{1,5},{5,9},{9,... | collective-permute-start | bytes 6152 | tf_op jit(solution)/shard_map/ppermute | solution.py:16
  106.9 1.3 collective-permute-done.8
  108.1 1.3 collective-permute-start.11
  109.4 3.0 %collective-permute-start.10 = (bf16[3,1,8,128]{3,2,1,0:T(8,128)(2,1)S(1)}, bf16[3,1,8,128]{3,2,1,0:T(8,128)(2,1)S(1)}, u32[]{:S(2)}, u32[]{:S(2)}) collective-permute-start(bf16[3,1,8,128]{3,2,1,0:T(8,128)(2,1)S(1)} %pad_maximum_fusion.6), channel_id=1, source_target_pairs={{0,1},{1,2},{2,3},{4,5},{5,6},{6,7},{8,9},{9,10},{10,11},{12,13},{... | collective-permute-start | bytes 18440 | tf_op jit(solution)/shard_map/ppermute | solution.py:16
  112.6 0.7 collective-permute-done.10
  113.3 0.6 gather_fusion.2
  114.0 0.4 fusion.2
  114.3 0.7 multiply_reduce_fusion.8
  115.0 1.9 pad_maximum_fusion.11
  116.9 8.1 %all-reduce.5 = (f32[]{:T(128)}, f32[3]{0:T(128)S(1)}) all-reduce(f32[]{:T(128)} %get-tuple-element.8, f32[3]{0:T(128)S(1)} %pad_maximum_fusion.11), channel_id=1, replica_groups=mesh['row'=8,'col'=4] {'col'}, use_global_device_ids=true, to_apply=%region_21.0 | all-reduce | flops 4 | bytes 32 | tf_op jit(solution)/shard_map/psum | solution.py:27
  125.0 20.0 %all-reduce.1 = (f32[]{:T(128)}, f32[3]{0:T(128)S(1)}) all-reduce(f32[]{:T(128)} %get-tuple-element.27, f32[3]{0:T(128)S(1)} %get-tuple-element.28), channel_id=1, replica_groups=mesh['row'=8,'col'=4] {'row'}, use_global_device_ids=true, to_apply=%region_22.0 | all-reduce | flops 4 | bytes 32 | tf_op jit(solution)/shard_map/psum | solution.py:28
  145.0 0.6 multiply_reduce_fusion.16
  145.6 0.6 fusion.20
  147.6 1.8 fusion.15
  149.5 1.3 collective-permute-start.13
  150.8 4.5 %collective-permute-start.12 = (bf16[1,1,8,128]{3,2,1,0:T(8,128)(2,1)S(1)}, bf16[1,1,8,128]{3,2,1,0:T(8,128)(2,1)S(1)}, u32[]{:S(2)}, u32[]{:S(2)}) collective-permute-start(bf16[1,1,8,128]{3,2,1,0:T(8,128)(2,1)S(1)} %get-tuple-element.33), channel_id=1, source_target_pairs={{0,4},{4,8},{8,12},{12,16},{16,20},{20,24},{24,28},{1,5},{5,9},{9,... | collective-permute-start | bytes 6152 | tf_op jit(solution)/shard_map/ppermute | solution.py:16
  155.4 1.2 collective-permute-done.12
  156.6 1.3 collective-permute-start.15
  157.9 3.0 %collective-permute-start.14 = (bf16[3,1,8,128]{3,2,1,0:T(8,128)(2,1)S(1)}, bf16[3,1,8,128]{3,2,1,0:T(8,128)(2,1)S(1)}, u32[]{:S(2)}, u32[]{:S(2)}) collective-permute-start(bf16[3,1,8,128]{3,2,1,0:T(8,128)(2,1)S(1)} %pad_maximum_fusion.7), channel_id=1, source_target_pairs={{0,1},{1,2},{2,3},{4,5},{5,6},{6,7},{8,9},{9,10},{10,11},{12,13},{... | collective-permute-start | bytes 18440 | tf_op jit(solution)/shard_map/ppermute | solution.py:16
  161.0 0.7 collective-permute-done.14
  161.7 0.6 gather_fusion.3
  162.4 0.4 fusion
  162.8 0.7 multiply_reduce_fusion.4
  163.5 2.6 %pad_maximum_fusion.12 = f32[4]{0:T(128)S(1)} fusion(f32[1]{0:T(128)} %bitcast.52, f32[1]{0:T(128)} %bitcast.51, f32[1]{0:T(128)} %bitcast.50, f32[1]{0:T(128)} %bitcast.49), kind=kLoop, calls=%fused_computation.72 | loop fusion | flops 12 | bytes 32 | tf_op jit(solution)/shard_map/stack | solution.py:81
  166.1 8.1 %all-reduce.4 = (f32[]{:T(128)}, f32[4]{0:T(128)S(1)}) all-reduce(f32[]{:T(128)} %get-tuple-element.3, f32[4]{0:T(128)S(1)} %pad_maximum_fusion.12), channel_id=1, replica_groups=mesh['row'=8,'col'=4] {'col'}, use_global_device_ids=true, to_apply=%region_31.0 | all-reduce | flops 5 | bytes 40 | tf_op jit(solution)/shard_map/psum | solution.py:27
  174.2 20.0 %all-reduce = (f32[]{:T(128)}, f32[4]{0:T(128)S(1)}) all-reduce(f32[]{:T(128)} %get-tuple-element.25, f32[4]{0:T(128)S(1)} %get-tuple-element.26), channel_id=1, replica_groups=mesh['row'=8,'col'=4] {'row'}, use_global_device_ids=true, to_apply=%region_32.0 | all-reduce | flops 5 | bytes 40 | tf_op jit(solution)/shard_map/psum | solution.py:28
  194.2 0.6 multiply_reduce_fusion.15
  196.4 0.4 copy-done.3
  196.9 0.4 cholesky.18
  197.3 0.6 compare_reduce_fusion
  198.0 0.6 select_select_fusion
  198.6 0.6 fusion.19
  199.2 0.7 fusion.18
  215.1 0.6 multiply_add_fusion
  (49 shorter events, 1.5 us)
Async XLA Ops:
  0.6 14.9 %copy-start = (bf16[1,1,8,4,128,128]{5,4,3,2,1,0:T(8,128)(2,1)S(1)}, bf16[1,1,8,4,128,128]{5,4,3,2,1,0:T(8,128)(2,1)}, u32[]{:S(2)}) copy-start(bf16[1,1,8,4,128,128]{5,4,3,2,1,0:T(8,128)(2,1)} %param.6) | copy-start | bytes 3145732
  0.6 7.8 %copy-start.5 = (s32[1,1,8]{2,1,0:T(1,128)S(1)}, s32[1,1,8]{2,1,0:T(1,128)}, u32[]{:S(2)}) copy-start(s32[1,1,8]{2,1,0:T(1,128)} %param.8) | copy-start | bytes 100
  1.4 7.0 %copy-start.4 = (s32[1,1,8,4]{2,3,1,0:T(4,128)S(1)}, s32[1,1,8,4]{2,3,1,0:T(4,128)}, u32[]{:S(2)}) copy-start(s32[1,1,8,4]{2,3,1,0:T(4,128)} %param.7) | copy-start | bytes 388
  1.4 7.2 %collective-permute-start.1 = (bf16[1,1,8,128]{3,2,1,0:T(8,128)(2,1)S(1)}, bf16[1,1,8,128]{3,2,1,0:T(8,128)(2,1)S(1)}, u32[]{:S(2)}, u32[]{:S(2)}) collective-permute-start(bf16[1,1,8,128]{3,2,1,0:T(8,128)(2,1)S(1)} %convert_element_type.19), channel_id=1, source_target_pairs={{4,0},{8,4},{12,8},{16,12},{20,16},{24,20},{28,24},{5,1},{9,5},{13... | collective-permute-start | bytes 6152 | tf_op jit(solution)/shard_map/ppermute | solution.py:17
  2.9 6.8 %collective-permute-start = (bf16[1,1,8,128]{3,2,1,0:T(8,128)(2,1)S(1)}, bf16[1,1,8,128]{3,2,1,0:T(8,128)(2,1)S(1)}, u32[]{:S(2)}, u32[]{:S(2)}) collective-permute-start(bf16[1,1,8,128]{3,2,1,0:T(8,128)(2,1)S(1)} %convert_element_type.19), channel_id=1, source_target_pairs={{0,4},{4,8},{8,12},{12,16},{16,20},{20,24},{24,28},{1,5},{5,9},{9,... | collective-permute-start | bytes 6152 | tf_op jit(solution)/shard_map/ppermute | solution.py:16
  9.7 4.3 %collective-permute-start.3 = (bf16[3,1,8,128]{3,2,1,0:T(8,128)(2,1)S(1)}, bf16[3,1,8,128]{3,2,1,0:T(8,128)(2,1)S(1)}, u32[]{:S(2)}, u32[]{:S(2)}) collective-permute-start(bf16[3,1,8,128]{3,2,1,0:T(8,128)(2,1)S(1)} %pad_maximum_fusion.4), channel_id=1, source_target_pairs={{1,0},{2,1},{3,2},{5,4},{6,5},{7,6},{9,8},{10,9},{11,10},{13,12},{... | collective-permute-start | bytes 18440 | tf_op jit(solution)/shard_map/ppermute | solution.py:17
  11.0 3.8 %collective-permute-start.2 = (bf16[3,1,8,128]{3,2,1,0:T(8,128)(2,1)S(1)}, bf16[3,1,8,128]{3,2,1,0:T(8,128)(2,1)S(1)}, u32[]{:S(2)}, u32[]{:S(2)}) collective-permute-start(bf16[3,1,8,128]{3,2,1,0:T(8,128)(2,1)S(1)} %pad_maximum_fusion.4), channel_id=1, source_target_pairs={{0,1},{1,2},{2,3},{4,5},{5,6},{6,7},{8,9},{9,10},{10,11},{12,13},{... | collective-permute-start | bytes 18440 | tf_op jit(solution)/shard_map/ppermute | solution.py:16
  15.5 0.7 copy-start.1
  15.5 0.7 copy-start.2
  53.6 5.9 %collective-permute-start.5 = (bf16[1,1,8,128]{3,2,1,0:T(8,128)(2,1)S(1)}, bf16[1,1,8,128]{3,2,1,0:T(8,128)(2,1)S(1)}, u32[]{:S(2)}, u32[]{:S(2)}) collective-permute-start(bf16[1,1,8,128]{3,2,1,0:T(8,128)(2,1)S(1)} %get-tuple-element.39), channel_id=1, source_target_pairs={{4,0},{8,4},{12,8},{16,12},{20,16},{24,20},{28,24},{5,1},{9,5},{13... | collective-permute-start | bytes 6152 | tf_op jit(solution)/shard_map/ppermute | solution.py:17
  54.9 5.8 %collective-permute-start.4 = (bf16[1,1,8,128]{3,2,1,0:T(8,128)(2,1)S(1)}, bf16[1,1,8,128]{3,2,1,0:T(8,128)(2,1)S(1)}, u32[]{:S(2)}, u32[]{:S(2)}) collective-permute-start(bf16[1,1,8,128]{3,2,1,0:T(8,128)(2,1)S(1)} %get-tuple-element.39), channel_id=1, source_target_pairs={{0,4},{4,8},{8,12},{12,16},{16,20},{20,24},{24,28},{1,5},{5,9},{9,... | collective-permute-start | bytes 6152 | tf_op jit(solution)/shard_map/ppermute | solution.py:16
  60.8 4.3 %collective-permute-start.7 = (bf16[3,1,8,128]{3,2,1,0:T(8,128)(2,1)S(1)}, bf16[3,1,8,128]{3,2,1,0:T(8,128)(2,1)S(1)}, u32[]{:S(2)}, u32[]{:S(2)}) collective-permute-start(bf16[3,1,8,128]{3,2,1,0:T(8,128)(2,1)S(1)} %pad_maximum_fusion.5), channel_id=1, source_target_pairs={{1,0},{2,1},{3,2},{5,4},{6,5},{7,6},{9,8},{10,9},{11,10},{13,12},{... | collective-permute-start | bytes 18440 | tf_op jit(solution)/shard_map/ppermute | solution.py:17
  62.1 3.8 %collective-permute-start.6 = (bf16[3,1,8,128]{3,2,1,0:T(8,128)(2,1)S(1)}, bf16[3,1,8,128]{3,2,1,0:T(8,128)(2,1)S(1)}, u32[]{:S(2)}, u32[]{:S(2)}) collective-permute-start(bf16[3,1,8,128]{3,2,1,0:T(8,128)(2,1)S(1)} %pad_maximum_fusion.5), channel_id=1, source_target_pairs={{0,1},{1,2},{2,3},{4,5},{5,6},{6,7},{8,9},{9,10},{10,11},{12,13},{... | collective-permute-start | bytes 18440 | tf_op jit(solution)/shard_map/ppermute | solution.py:16
  101.0 5.9 %collective-permute-start.9 = (bf16[1,1,8,128]{3,2,1,0:T(8,128)(2,1)S(1)}, bf16[1,1,8,128]{3,2,1,0:T(8,128)(2,1)S(1)}, u32[]{:S(2)}, u32[]{:S(2)}) collective-permute-start(bf16[1,1,8,128]{3,2,1,0:T(8,128)(2,1)S(1)} %get-tuple-element.36), channel_id=1, source_target_pairs={{4,0},{8,4},{12,8},{16,12},{20,16},{24,20},{28,24},{5,1},{9,5},{13... | collective-permute-start | bytes 6152 | tf_op jit(solution)/shard_map/ppermute | solution.py:17
  102.3 5.8 %collective-permute-start.8 = (bf16[1,1,8,128]{3,2,1,0:T(8,128)(2,1)S(1)}, bf16[1,1,8,128]{3,2,1,0:T(8,128)(2,1)S(1)}, u32[]{:S(2)}, u32[]{:S(2)}) collective-permute-start(bf16[1,1,8,128]{3,2,1,0:T(8,128)(2,1)S(1)} %get-tuple-element.36), channel_id=1, source_target_pairs={{0,4},{4,8},{8,12},{12,16},{16,20},{20,24},{24,28},{1,5},{5,9},{9,... | collective-permute-start | bytes 6152 | tf_op jit(solution)/shard_map/ppermute | solution.py:16
  108.1 4.4 %collective-permute-start.11 = (bf16[3,1,8,128]{3,2,1,0:T(8,128)(2,1)S(1)}, bf16[3,1,8,128]{3,2,1,0:T(8,128)(2,1)S(1)}, u32[]{:S(2)}, u32[]{:S(2)}) collective-permute-start(bf16[3,1,8,128]{3,2,1,0:T(8,128)(2,1)S(1)} %pad_maximum_fusion.6), channel_id=1, source_target_pairs={{1,0},{2,1},{3,2},{5,4},{6,5},{7,6},{9,8},{10,9},{11,10},{13,12},{... | collective-permute-start | bytes 18440 | tf_op jit(solution)/shard_map/ppermute | solution.py:17
  109.4 3.8 %collective-permute-start.10 = (bf16[3,1,8,128]{3,2,1,0:T(8,128)(2,1)S(1)}, bf16[3,1,8,128]{3,2,1,0:T(8,128)(2,1)S(1)}, u32[]{:S(2)}, u32[]{:S(2)}) collective-permute-start(bf16[3,1,8,128]{3,2,1,0:T(8,128)(2,1)S(1)} %pad_maximum_fusion.6), channel_id=1, source_target_pairs={{0,1},{1,2},{2,3},{4,5},{5,6},{6,7},{8,9},{9,10},{10,11},{12,13},{... | collective-permute-start | bytes 18440 | tf_op jit(solution)/shard_map/ppermute | solution.py:16
  149.5 5.9 %collective-permute-start.13 = (bf16[1,1,8,128]{3,2,1,0:T(8,128)(2,1)S(1)}, bf16[1,1,8,128]{3,2,1,0:T(8,128)(2,1)S(1)}, u32[]{:S(2)}, u32[]{:S(2)}) collective-permute-start(bf16[1,1,8,128]{3,2,1,0:T(8,128)(2,1)S(1)} %get-tuple-element.33), channel_id=1, source_target_pairs={{4,0},{8,4},{12,8},{16,12},{20,16},{24,20},{28,24},{5,1},{9,5},{13... | collective-permute-start | bytes 6152 | tf_op jit(solution)/shard_map/ppermute | solution.py:17
  150.8 5.8 %collective-permute-start.12 = (bf16[1,1,8,128]{3,2,1,0:T(8,128)(2,1)S(1)}, bf16[1,1,8,128]{3,2,1,0:T(8,128)(2,1)S(1)}, u32[]{:S(2)}, u32[]{:S(2)}) collective-permute-start(bf16[1,1,8,128]{3,2,1,0:T(8,128)(2,1)S(1)} %get-tuple-element.33), channel_id=1, source_target_pairs={{0,4},{4,8},{8,12},{12,16},{16,20},{20,24},{24,28},{1,5},{5,9},{9,... | collective-permute-start | bytes 6152 | tf_op jit(solution)/shard_map/ppermute | solution.py:16
  156.6 4.4 %collective-permute-start.15 = (bf16[3,1,8,128]{3,2,1,0:T(8,128)(2,1)S(1)}, bf16[3,1,8,128]{3,2,1,0:T(8,128)(2,1)S(1)}, u32[]{:S(2)}, u32[]{:S(2)}) collective-permute-start(bf16[3,1,8,128]{3,2,1,0:T(8,128)(2,1)S(1)} %pad_maximum_fusion.7), channel_id=1, source_target_pairs={{1,0},{2,1},{3,2},{5,4},{6,5},{7,6},{9,8},{10,9},{11,10},{13,12},{... | collective-permute-start | bytes 18440 | tf_op jit(solution)/shard_map/ppermute | solution.py:17
  157.9 3.8 %collective-permute-start.14 = (bf16[3,1,8,128]{3,2,1,0:T(8,128)(2,1)S(1)}, bf16[3,1,8,128]{3,2,1,0:T(8,128)(2,1)S(1)}, u32[]{:S(2)}, u32[]{:S(2)}) collective-permute-start(bf16[3,1,8,128]{3,2,1,0:T(8,128)(2,1)S(1)} %pad_maximum_fusion.7), channel_id=1, source_target_pairs={{0,1},{1,2},{2,3},{4,5},{5,6},{6,7},{8,9},{9,10},{10,11},{12,13},{... | collective-permute-start | bytes 18440 | tf_op jit(solution)/shard_map/ppermute | solution.py:16
  196.3 0.6 copy-start.3
where the time goes:
time: 217 us; the launch traced here: 216 us
  blocking collectives  116 us (53%)
  starting transfers between devices  41.7 us (19%)
  between operations  23.7 us (11%)
  other arithmetic  18.6 us (9%)
  waiting for transfers between devices  7.84 us (4%)
  local copies, waits for them, and re-layouts  6.53 us (3%)
    psum x4, blocking collectives, global_sum(): return lax.psum((partial_dots, partial_square), 'row')  83.2 us
    psum x4, blocking collectives, global_sum(): partial_dots, partial_square = lax.psum((dot_terms, square_term), 'col')  32.5 us
    ppermute x8, starting transfers between devices, padded(): before = lax.ppermute(last, axis, up)  31.3 us
    ppermute x8, starting transfers between devices, padded(): after = lax.ppermute(first, axis, down)  10.4 us
    ppermute x8, waiting for transfers between devices, padded(): before = lax.ppermute(last, axis, up)  7.82 us
    another operation x3, other arithmetic, on_device(): local_proj = jnp.stack([jnp.sum(vector * residue) for vector in basis])  5.78 us
  transfers between devices with their start and end apart: 16, of which 8 were waited for; matrix products, arithmetic and copies ran while one was open for 0% of the time, Pallas kernels for 0%

commit v1 on v0

v1 whole, which is shorter than its diff:
```python
import functools

import jax
import jax.numpy as jnp
from jax import lax
from jax.experimental import pallas as pl
from jax.experimental.pallas import tpu as pltpu
from jax.sharding import PartitionSpec as P

ITERS = 4
MESH = pl.DeviceIdType.MESH
UNROLL_LIMIT = 64


def kernel(n_row, n_col, cols_ref, live_ref, rhs_hbm, scale_hbm, vals_hbm,
           field_ref, hess_ref,
           vals, scale, first, later, basis, dots, pieces, index,
           load_sem, vals_sem, halo_send, halo_recv, dot_send, dot_recv):
    f32 = jnp.float32
    row, col = lax.axis_index("row"), lax.axis_index("col")
    n_dev = n_row * n_col
    me = row * n_col + col
    blocks, slots, size = vals.shape[0], vals.shape[1], vals.shape[2]
    barrier = pltpu.get_barrier_semaphore()

    def field(stage):
        return first if stage == 0 else later.at[stage - 1]

    def part(stage, k):
        return field(stage).at[pl.ds(k * blocks, blocks)]

    load_rhs = pltpu.make_async_copy(rhs_hbm.at[0, 0], part(0, 4), load_sem.at[0])
    load_rhs.start()
    load_scale = pltpu.make_async_copy(scale_hbm.at[0, 0], scale, load_sem.at[1])
    load_scale.start()
    load_vals = [
        pltpu.make_async_copy(vals_hbm.at[0, 0, n], vals.at[n], vals_sem.at[n])
        for n in range(blocks)
    ]
    for copy in load_vals:
        copy.start()

    for stage in range(ITERS):
        for k in range(10):
            if k != 4:
                part(stage, k)[...] = jnp.zeros((blocks, size), f32)
    for n in range(blocks):
        for s in range(slots):
            index[n * slots + s] = jnp.where(
                s < live_ref[0, 0, n], cols_ref[0, 0, s, n], 9 * blocks)

    def others(act):
        if n_dev <= UNROLL_LIMIT:
            steps = sorted(range(1, n_dev), key=lambda t: abs(t - n_dev / 2))
            for t in steps:
                act((lax.rem(row + t // n_col, n_row), lax.rem(col + t % n_col, n_col)))
        else:
            def body(t, carry):
                act((lax.rem(row + t // n_col, n_row), lax.rem(col + t % n_col, n_col)))
                return carry
            lax.fori_loop(1, n_dev, body, 0)

    others(lambda where: pl.semaphore_signal(barrier, inc=1, device_id=where, device_id_type=MESH))
    pl.semaphore_wait(barrier, n_dev - 1)

    around = [(k, k // 3 - 1, k % 3 - 1) for k in range(9) if k != 4]

    def inside(a, b):
        ok = None
        for at, count, shift in ((row, n_row, a), (col, n_col, b)):
            if shift:
                here = (at > 0) if shift < 0 else (at < count - 1)
                ok = here if ok is None else jnp.logical_and(ok, here)
        return ok

    def halo_copy(stage, k, a, b):
        return pltpu.make_async_remote_copy(
            src_ref=part(stage, 4), dst_ref=part(stage, 8 - k),
            send_sem=halo_send.at[stage, k], recv_sem=halo_recv.at[stage, 8 - k],
            device_id=(row + a, col + b), device_id_type=MESH)

    def halo_start(stage):
        for k, a, b in around:
            @pl.when(inside(a, b))
            def _():
                halo_copy(stage, k, a, b).start()

    def halo_wait(stage):
        for k, a, b in around:
            @pl.when(inside(a, b))
            def _():
                pltpu.make_async_copy(
                    part(stage, k), part(stage, k), halo_recv.at[stage, k]).wait()

    def halo_done(stage):
        for k, a, b in around:
            @pl.when(inside(a, b))
            def _():
                pltpu.make_async_copy(
                    part(stage, 4), part(stage, 4), halo_send.at[stage, k]).wait()

    lane = lax.broadcasted_iota(jnp.int32, (1, size), 1)

    def reduce_start(stage, products):
        line = jnp.zeros((1, size), f32)
        for i, product in enumerate(products):
            line = jnp.where(lane == i, jnp.sum(product, keepdims=True), line)
        dots[stage, me] = line
        others(lambda where: pltpu.make_async_remote_copy(
            src_ref=dots.at[stage, me], dst_ref=dots.at[stage, me],
            send_sem=dot_send.at[stage], recv_sem=dot_recv.at[stage],
            device_id=where, device_id_type=MESH).start())

    def all_bytes(stage, sem):
        most = dots.at[stage, pl.ds(0, n_dev - 1)]
        return pltpu.make_async_copy(most, most, sem.at[stage])

    def reduce_wait(stage, count):
        all_bytes(stage, dot_recv).wait()
        if n_dev <= UNROLL_LIMIT:
            lines = [dots[stage, d] for d in range(n_dev)]
            while len(lines) > 1:
                lines = [sum(lines[i:i + 2]) for i in range(0, len(lines), 2)]
            total = lines[0]
        else:
            total = lax.fori_loop(
                0, n_dev, lambda d, acc: acc + dots[stage, d], jnp.zeros((1, size), f32))
        return [jnp.broadcast_to(total[:, i:i + 1], (blocks, size)) for i in range(count)]

    def operate(source, own):
        for n in range(blocks):
            for s in range(slots):
                pieces[n:n + 1, s * size:(s + 1) * size] = source[
                    pl.ds(index[n * slots + s], 1), :]
        left = pieces[...].astype(jnp.bfloat16)
        out = []
        for n in range(0, blocks, 2):
            acc = jnp.zeros((blocks, 2 * size), f32)
            for s in range(0, slots, 2):
                right = jnp.concatenate([
                    jnp.concatenate([vals[n + d, s], vals[n + d, s + 1]], axis=1)
                    for d in range(2)], axis=0)
                acc = acc + lax.dot_general(
                    left[:, s * size:(s + 2) * size], right,
                    (((1,), (1,)), ((), ())), preferred_element_type=f32)
            out.append(acc[n:n + 1, :size])
            out.append(acc[n + 1:n + 2, size:])
        return scale[...] * own + jnp.concatenate(out, axis=0)

    load_rhs.wait()
    halo_start(0)
    load_scale.wait()
    halo_wait(0)
    for copy in load_vals:
        copy.wait()
    own = pl.ds(4 * blocks, blocks)
    rhs = first[own, :]
    image = operate(first, rhs)
    later[0, own, :] = image
    reduce_start(0, [rhs * rhs, rhs * image, image * image])
    halo_start(1)

    def tall(x):
        return jnp.concatenate([x] * 10, axis=0)

    columns = []
    gram = [[None] * ITERS for _ in range(ITERS)]
    factor = [[None] * ITERS for _ in range(ITERS)]
    inverse = [None] * ITERS
    forward = []
    for j in range(ITERS):
        if j == 0:
            self_dot, cross_dot, image_dot = reduce_wait(0, 3)
            norm = jnp.sqrt(self_dot)
            inv_norm = 1.0 / norm
            inv_self = 1.0 / self_dot
            proj = [cross_dot * inv_self]
            square = image_dot * inv_self
        else:
            got = reduce_wait(j, j + 2)
            proj, square = got[:j + 1], got[j + 1]
        total = proj[0] * proj[0]
        for h in proj[1:]:
            total = total + h * h
        height = jnp.sqrt(square - total)
        if j + 1 < ITERS:
            halo_wait(j + 1)
            inv_height = 1.0 / height
            if j == 0:
                wide_norm = tall(inv_norm)
                basis[0] = first[...] * wide_norm
                w = later[0] * wide_norm
            else:
                w = later[j]
            for i in range(j + 1):
                w = w - tall(proj[i]) * basis[i]
            basis[j + 1] = w * tall(inv_height)
            here = [basis[i, own, :] for i in range(j + 2)]
            image = operate(basis.at[j + 1], here[-1])
            if j + 2 < ITERS:
                later[j + 1, own, :] = image
            reduce_start(j + 1, [v * image for v in here] + [image * image])
            if j + 2 < ITERS:
                halo_start(j + 2)
        columns.append(proj + [height])
        for i in range(j + 1):
            acc = columns[i][0] * columns[j][0]
            for m in range(1, i + 2):
                acc = acc + columns[i][m] * columns[j][m]
            gram[j][i] = acc
        for i in range(j + 1):
            acc = gram[j][i]
            for m in range(i):
                acc = acc - factor[j][m] * factor[i][m]
            if i == j:
                factor[j][j] = jnp.sqrt(acc)
                inverse[j] = 1.0 / factor[j][j]
            else:
                factor[j][i] = acc * inverse[i]
        acc = norm * columns[j][0]
        for m in range(j):
            acc = acc - factor[j][m] * forward[m]
        forward.append(acc * inverse[j])
    weights = [None] * ITERS
    for i in reversed(range(ITERS)):
        acc = forward[i]
        for m in range(i + 1, ITERS):
            acc = acc - factor[m][i] * weights[m]
        weights[i] = acc * inverse[i]
    result = weights[0] * basis[0, own, :]
    for i in range(1, ITERS):
        result = result + weights[i] * basis[i, own, :]
    field_ref[0, 0] = result
    down = lax.broadcasted_iota(jnp.int32, (blocks, size), 0)
    along = lax.broadcasted_iota(jnp.int32, (blocks, size), 1)
    hess = jnp.zeros((blocks, size), f32)
    for j in range(ITERS):
        for i in range(j + 2):
            hess = jnp.where((down == j) & (along == i), columns[j][i], hess)
    hess_ref[...] = hess[:ITERS, :ITERS + 1]
    for stage in range(ITERS):
        all_bytes(stage, dot_send).wait()
        halo_done(stage)


def on_device(right_side, block_values, block_columns, live_slots, row_scale):
    n_row, n_col = lax.axis_size("row"), lax.axis_size("col")
    blocks, slots, size = block_values.shape[2:5]
    f32 = jnp.float32
    result, hess = pl.pallas_call(
        functools.partial(kernel, n_row, n_col),
        out_shape=(
            jax.ShapeDtypeStruct(right_side.shape, f32),
            jax.ShapeDtypeStruct((ITERS, ITERS + 1), f32),
        ),
        in_specs=[pl.BlockSpec(memory_space=pltpu.SMEM)] * 2
        + [pl.BlockSpec(memory_space=pltpu.HBM)] * 3,
        out_specs=(pl.BlockSpec(memory_space=pltpu.VMEM),) * 2,
        scratch_shapes=[
            pltpu.VMEM((blocks, slots, size, size), jnp.bfloat16),
            pltpu.VMEM((blocks, size), f32),
            pltpu.VMEM((10 * blocks, size), f32),
            pltpu.VMEM((ITERS - 1, 10 * blocks, size), f32),
            pltpu.VMEM((ITERS, 10 * blocks, size), f32),
            pltpu.VMEM((ITERS, n_row * n_col, 1, size), f32),
            pltpu.VMEM((blocks, slots * size), f32),
            pltpu.SMEM((blocks * slots,), jnp.int32),
            pltpu.SemaphoreType.DMA((2,)),
            pltpu.SemaphoreType.DMA((blocks,)),
            pltpu.SemaphoreType.DMA((ITERS, 9)),
            pltpu.SemaphoreType.DMA((ITERS, 9)),
            pltpu.SemaphoreType.DMA((ITERS,)),
            pltpu.SemaphoreType.DMA((ITERS,)),
        ],
        compiler_params=pltpu.CompilerParams(
            collective_id=0, has_side_effects=True, vmem_limit_bytes=67_043_328),
    )(block_columns.swapaxes(2, 3), live_slots, right_side, row_scale, block_values)
    return result, hess.T


def solution(mesh):
    return jax.shard_map(
        on_device,
        mesh=mesh,
        in_specs=(
            P("row", "col", None, None),
            P("row", "col", None, None, None, None),
            P("row", "col", None, None),
            P("row", "col", None),
            P("row", "col", None, None),
        ),
        out_specs=(P("row", "col", None, None), P()),
        check_vma=False,
    )
```

time: 217 us -> 34.6 us (0.16)
  blocking collectives: 116 us -> 0 us
  starting transfers between devices: 41.7 us -> 0 us
  Pallas kernels: 0 us -> 31.9 us
  between operations: 23.7 us -> 0.65 us
  other arithmetic: 18.6 us -> 0 us
  waiting for transfers between devices: 7.84 us -> 0 us
  local copies, waits for them, and re-layouts: 6.53 us -> 1.91 us
    psum x8 -> x0, blocking collectives: 116 us -> none  [the longest x4 83.2 us: global_sum(): return lax.psum((partial_dots, partial_square), 'row')]
    ppermute x16 -> x0, starting transfers between devices: 41.7 us -> none  [the longest x8 31.3 us: padded(): before = lax.ppermute(last, axis, up)]
    pallas_call x0 -> x1, Pallas kernels: none -> 31.9 us  [on_device(): pl.pallas_call(functools.partial(kernel, n_row, n_col), out_shape=(jax.Sh...]
    another operation x12 -> x0, other arithmetic: 8.49 us -> none  [the longest x3 5.78 us: on_device(): local_proj = jnp.stack([jnp.sum(vector * residue) for vector in basis])]
    ppermute x16 -> x0, waiting for transfers between devices: 7.84 us -> none  [the longest x8 7.82 us: padded(): before = lax.ppermute(last, axis, up)]
    reduce_sum x7 -> x0, other arithmetic: 4.64 us -> none  [the longest x3 2.09 us: on_device(): local_proj = jnp.stack([jnp.sum(vector * residue) for vector in basis])]
    convert_element_type x5 -> x0, other arithmetic: 3.9 us -> none  [the longest x4 3.83 us: operate(): rounded = field.astype(jnp.bfloat16)]
    slice x5 -> x0, local copies, waits for them, and re-layouts: 3.12 us -> none  [the longest x2 1.26 us: on_device(): residue = residue - projections[ordinal] * basis[ordinal]]
  transfers between devices with their start and end apart: 16 -> 0, of which waited for: 8 -> 0; matrix products, arithmetic and copies ran while one was open for 0% -> 0% of each run, Pallas kernels for 0% -> 0%
where the time goes in v1:
time: 34.6 us; the launch traced here: 34.4 us
  Pallas kernels  31.9 us (92%)
  local copies, waits for them, and re-layouts  1.91 us (6%)
  between operations  0.65 us (2%)
    pallas_call x1, Pallas kernels, on_device(): pl.pallas_call(functools.partial(kernel, n_row, n_col), out_shape=(jax.Sh...  31.9 us
    unnamed x6, local copies, waits for them, and re-layouts  1.91 us

profile of v1, /device:TPU:0, one launch (start us, length us, event | category | flops | bytes accessed | tf_op | source)
XLA Modules:
  0.0 34.4 jit_solution(16896388141102026252)
XLA Ops:
  0.6 31.9 %shard_map.68 = (f32[1,1,8,128]{3,2,1,0:T(8,128)}, f32[4,5]{1,0:T(4,128)}) custom-call(s32[1,1,4,8]{3,2,1,0:T(4,128)} %bitcast.2, s32[1,1,8]{2,1,0:T(1,128)} %live_ref.1, f32[1,1,8,128]{3,2,1,0:T(8,128)} %rhs_hbm.1, f32[1,1,8,128]{3,2,1,0:T(8,128)} %scale_hbm.1, bf16[1,1,8,4,128,128]{5,4,3,2,1,0:T(8,128)(2,1)} %vals_hbm.1), custom_call_target="tpu_custom_call" | custom-call | tf_op jit(solution)/shard_map/pallas_call | solution.py:250
  32.5 0.0 copy-start
  32.5 0.7 %copy-done = f32[1,1,8,128]{3,2,1,0:T(8,128)S(1)} copy-done((f32[1,1,8,128]{3,2,1,0:T(8,128)S(1)}, f32[1,1,8,128]{3,2,1,0:T(8,128)}, u32[]{:S(2)}) %copy-start) | copy-done | bytes 4120
  33.2 0.0 copy-start.1
  33.2 0.6 %copy.9 = f32[1,1,8,128]{3,2,1,0:T(8,128)} copy(f32[1,1,8,128]{3,2,1,0:T(8,128)S(1)} %copy-done) | data formatting | bytes 8192
  33.8 0.1 copy-done.1
  33.8 0.6 %copy.10 = f32[5,4]{0,1:T(4,128)} copy(f32[5,4]{0,1:T(4,128)S(1)} %bitcast.3) | data formatting | bytes 160
Async XLA Ops:
  32.5 0.7 %copy-start = (f32[1,1,8,128]{3,2,1,0:T(8,128)S(1)}, f32[1,1,8,128]{3,2,1,0:T(8,128)}, u32[]{:S(2)}) copy-start(f32[1,1,8,128]{3,2,1,0:T(8,128)} %get-tuple-element.8) | copy-start | bytes 12292
  33.2 0.7 %copy-start.1 = (f32[4,5]{1,0:T(4,128)S(1)}, f32[4,5]{1,0:T(4,128)}, u32[]{:S(2)}) copy-start(f32[4,5]{1,0:T(4,128)} %get-tuple-element.5) | copy-start | bytes 244

commit v2 on v1

--- a/solution.py
+++ b/solution.py
@@ -15,7 +15,8 @@
 def kernel(n_row, n_col, cols_ref, live_ref, rhs_hbm, scale_hbm, vals_hbm,
            field_ref, hess_ref,
            vals, scale, first, later, basis, dots, pieces, index,
-           load_sem, vals_sem, halo_send, halo_recv, dot_send, dot_recv):
+           load_sem, vals_sem, halo_send, halo_recv, dot_send, dot_recv,
+           meet_sem):
     f32 = jnp.float32
     row, col = lax.axis_index("row"), lax.axis_index("col")
     n_dev = n_row * n_col
@@ -44,10 +45,6 @@
         for k in range(10):
             if k != 4:
                 part(stage, k)[...] = jnp.zeros((blocks, size), f32)
-    for n in range(blocks):
-        for s in range(slots):
-            index[n * slots + s] = jnp.where(
-                s < live_ref[0, 0, n], cols_ref[0, 0, s, n], 9 * blocks)
 
     def others(act):
         if n_dev <= UNROLL_LIMIT:
@@ -60,18 +57,32 @@
                 return carry
             lax.fori_loop(1, n_dev, body, 0)
 
-    others(lambda where: pl.semaphore_signal(barrier, inc=1, device_id=where, device_id_type=MESH))
-    pl.semaphore_wait(barrier, n_dev - 1)
-
     around = [(k, k // 3 - 1, k % 3 - 1) for k in range(9) if k != 4]
 
     def inside(a, b):
         ok = None
         for at, count, shift in ((row, n_row, a), (col, n_col, b)):
             if shift:
-                here = (at > 0) if shift < 0 else (at < count - 1)
+                here = (at >= -shift) if shift < 0 else (at < count - shift)
                 ok = here if ok is None else jnp.logical_and(ok, here)
         return ok
+
+    def greet(sem, reach):
+        for _, a, b in around:
+            @pl.when(inside(a * reach, b * reach))
+            def _():
+                pl.semaphore_signal(
+                    sem, inc=1, device_id=(row + a * reach, col + b * reach),
+                    device_id_type=MESH)
+
+    def meet(sem, reach):
+        count = 1
+        for at, length in ((row, n_row), (col, n_col)):
+            count = count * (1 + (at >= reach).astype(jnp.int32)
+                             + (at < length - reach).astype(jnp.int32))
+        pl.semaphore_wait(sem, count - 1)
+
+    greet(barrier, 1)
 
     def halo_copy(stage, k, a, b):
         return pltpu.make_async_remote_copy(
@@ -147,16 +158,28 @@
             out.append(acc[n + 1:n + 2, size:])
         return scale[...] * own + jnp.concatenate(out, axis=0)
 
+    reaches = greetings(n_row, n_col)
+    for n in range(blocks):
+        for s in range(slots):
+            index[n * slots + s] = jnp.where(
+                s < live_ref[0, 0, n], cols_ref[0, 0, s, n], 9 * blocks)
     load_rhs.wait()
+    meet(barrier, 1)
     halo_start(0)
+    for i, reach in enumerate(reaches):
+        greet(meet_sem.at[i], reach)
+        if i + 1 < len(reaches):
+            meet(meet_sem.at[i], reach)
     load_scale.wait()
-    halo_wait(0)
     for copy in load_vals:
         copy.wait()
+    halo_wait(0)
     own = pl.ds(4 * blocks, blocks)
     rhs = first[own, :]
     image = operate(first, rhs)
     later[0, own, :] = image
+    if reaches:
+        meet(meet_sem.at[len(reaches) - 1], reaches[-1])
     reduce_start(0, [rhs * rhs, rhs * image, image * image])
     halo_start(1)
 
@@ -243,6 +266,25 @@
         halo_done(stage)
 
 
+def greetings(n_row, n_col):
+    reaches, reach = [], 1
+    while reach < max(n_row, n_col) - 1:
+        reaches.append(reach)
+        reach *= 2
+    return reaches
+
+
+def write_out(field_ref, hess_ref, field_out, hess_out, sems):
+    copies = [
+        pltpu.make_async_copy(field_ref, field_out, sems.at[0]),
+        pltpu.make_async_copy(hess_ref, hess_out, sems.at[1]),
+    ]
+    for copy in copies:
+        copy.start()
+    for copy in copies:
+        copy.wait()
+
+
 def on_device(right_side, block_values, block_columns, live_slots, row_scale):
     n_row, n_col = lax.axis_size("row"), lax.axis_size("col")
     blocks, slots, size = block_values.shape[2:5]
@@ -250,8 +292,8 @@
     result, hess = pl.pallas_call(
         functools.partial(kernel, n_row, n_col),
         out_shape=(
-            jax.ShapeDtypeStruct(right_side.shape, f32),
-            jax.ShapeDtypeStruct((ITERS, ITERS + 1), f32),
+            pltpu.VMEM(right_side.shape, f32),
+            pltpu.VMEM((ITERS, ITERS + 1), f32),
         ),
         in_specs=[pl.BlockSpec(memory_space=pltpu.SMEM)] * 2
         + [pl.BlockSpec(memory_space=pltpu.HBM)] * 3,
@@ -271,10 +313,24 @@
             pltpu.SemaphoreType.DMA((ITERS, 9)),
             pltpu.SemaphoreType.DMA((ITERS,)),
             pltpu.SemaphoreType.DMA((ITERS,)),
+            pltpu.SemaphoreType.REGULAR((max(1, len(greetings(n_row, n_col))),)),
         ],
         compiler_params=pltpu.CompilerParams(
-            collective_id=0, has_side_effects=True, vmem_limit_bytes=67_043_328),
-    )(block_columns.swapaxes(2, 3), live_slots, right_side, row_scale, block_values)
+            collective_id=0, has_side_effects=True, vmem_limit_bytes=60 << 20),
+    )(block_columns.swapaxes(2, 3), live_slots, *[
+        pltpu.with_memory_space_constraint(x, pltpu.HBM)
+        for x in (right_side, row_scale, block_values)])
+    result, hess = pl.pallas_call(
+        write_out,
+        out_shape=(
+            jax.ShapeDtypeStruct(right_side.shape, f32),
+            jax.ShapeDtypeStruct((ITERS, ITERS + 1), f32),
+        ),
+        in_specs=[pl.BlockSpec(memory_space=pltpu.VMEM)] * 2,
+        out_specs=[pl.BlockSpec(memory_space=pltpu.HBM)] * 2,
+        scratch_shapes=[pltpu.SemaphoreType.DMA((2,))],
+        compiler_params=pltpu.CompilerParams(vmem_limit_bytes=1 << 20),
+    )(result, hess)
     return result, hess.T
 
 

time: 34.6 us -> 33.1 us (0.957)
  local copies, waits for them, and re-layouts: 1.91 us -> 0 us
  Pallas kernels: 31.9 us -> 32.3 us
    unnamed x6 -> x0, local copies, waits for them, and re-layouts: 1.91 us -> none
    pallas_call x1 -> x2, Pallas kernels: 31.9 us -> 32.3 us  [the longest x1 31.7 us: on_device(): pl.pallas_call(functools.partial(kernel, n_row, n_col), out_shape=(pltpu....]
where the time goes in v2:
time: 33.1 us; the launch traced here: 32.9 us
  Pallas kernels  32.3 us (98%)
  between operations  0.64 us (2%)
    pallas_call x1, Pallas kernels, on_device(): pl.pallas_call(functools.partial(kernel, n_row, n_col), out_shape=(pltpu....  31.7 us

profile of v2, /device:TPU:0, one launch (start us, length us, event | category | flops | bytes accessed | tf_op | source)
XLA Modules:
  0.0 32.9 jit_solution(3377473862318268787)
XLA Ops:
  0.6 31.7 %shard_map.68 = (f32[1,1,8,128]{3,2,1,0:T(8,128)S(1)}, f32[4,5]{1,0:T(4,128)S(1)}) custom-call(s32[1,1,4,8]{3,2,1,0:T(4,128)} %bitcast.2, s32[1,1,8]{2,1,0:T(1,128)} %live_ref.1, f32[1,1,8,128]{3,2,1,0:T(8,128)} %rhs_hbm.1, f32[1,1,8,128]{3,2,1,0:T(8,128)} %scale_hbm.1, bf16[1,1,8,4,128,128]{5,4,3,2,1,0:T(8,128)(2,1)} %vals_hbm.1), custom_call_target="tpu_custom_call" | custom-call | tf_op jit(solution)/shard_map/pallas_call | solution.py:292
  32.3 0.6 %shard_map.69 = (f32[1,1,8,128]{3,2,1,0:T(8,128)}, f32[4,5]{1,0:T(4,128)}) custom-call(f32[1,1,8,128]{3,2,1,0:T(8,128)S(1)} %get-tuple-element.6.field_ref, f32[4,5]{1,0:T(4,128)S(1)} %get-tuple-element.7.hess_ref), custom_call_target="tpu_custom_call" | custom-call | tf_op jit(solution)/shard_map/pallas_call | solution.py:323

commit v3 on v2

--- a/solution.py
+++ b/solution.py
@@ -10,6 +10,7 @@
 ITERS = 4
 MESH = pl.DeviceIdType.MESH
 UNROLL_LIMIT = 64
+REACH = 2
 
 
 def kernel(n_row, n_col, cols_ref, live_ref, rhs_hbm, scale_hbm, vals_hbm,
@@ -67,22 +68,32 @@
                 ok = here if ok is None else jnp.logical_and(ok, here)
         return ok
 
+    def welcome():
+        for a in range(-REACH, REACH + 1):
+            def send(a=a):
+                for c in range(1 if a == 0 else 0, n_col):
+                    pl.semaphore_signal(
+                        barrier, inc=1, device_id=(row + a, lax.rem(col + c, n_col)),
+                        device_id_type=MESH)
+            if a == 0:
+                send()
+            else:
+                pl.when(inside(a, 0))(send)
+
+    def rows_at(reach):
+        return (row >= reach).astype(jnp.int32) + (row < n_row - reach).astype(jnp.int32)
+
     def greet(sem, reach):
-        for _, a, b in around:
-            @pl.when(inside(a * reach, b * reach))
+        for shift in (-reach, reach):
+            @pl.when(inside(shift, 0))
             def _():
                 pl.semaphore_signal(
-                    sem, inc=1, device_id=(row + a * reach, col + b * reach),
-                    device_id_type=MESH)
+                    sem, inc=1, device_id=(row + shift, col), device_id_type=MESH)
 
     def meet(sem, reach):
-        count = 1
-        for at, length in ((row, n_row), (col, n_col)):
-            count = count * (1 + (at >= reach).astype(jnp.int32)
-                             + (at < length - reach).astype(jnp.int32))
-        pl.semaphore_wait(sem, count - 1)
-
-    greet(barrier, 1)
+        pl.semaphore_wait(sem, rows_at(reach))
+
+    welcome()
 
     def halo_copy(stage, k, a, b):
         return pltpu.make_async_remote_copy(
@@ -158,13 +169,16 @@
             out.append(acc[n + 1:n + 2, size:])
         return scale[...] * own + jnp.concatenate(out, axis=0)
 
-    reaches = greetings(n_row, n_col)
+    reaches = greetings(n_row)
     for n in range(blocks):
         for s in range(slots):
             index[n * slots + s] = jnp.where(
                 s < live_ref[0, 0, n], cols_ref[0, 0, s, n], 9 * blocks)
     load_rhs.wait()
-    meet(barrier, 1)
+    near = 1
+    for reach in range(1, REACH + 1):
+        near = near + rows_at(reach)
+    pl.semaphore_wait(barrier, near * n_col - 1)
     halo_start(0)
     for i, reach in enumerate(reaches):
         greet(meet_sem.at[i], reach)
@@ -192,6 +206,10 @@
     inverse = [None] * ITERS
     forward = []
     for j in range(ITERS):
+        all_bytes(j, dot_send).wait()
+        halo_done(j)
+        if j + 1 < ITERS:
+            halo_wait(j + 1)
         if j == 0:
             self_dot, cross_dot, image_dot = reduce_wait(0, 3)
             norm = jnp.sqrt(self_dot)
@@ -207,7 +225,6 @@
             total = total + h * h
         height = jnp.sqrt(square - total)
         if j + 1 < ITERS:
-            halo_wait(j + 1)
             inv_height = 1.0 / height
             if j == 0:
                 wide_norm = tall(inv_norm)
@@ -261,14 +278,11 @@
         for i in range(j + 2):
             hess = jnp.where((down == j) & (along == i), columns[j][i], hess)
     hess_ref[...] = hess[:ITERS, :ITERS + 1]
-    for stage in range(ITERS):
-        all_bytes(stage, dot_send).wait()
-        halo_done(stage)
-
-
-def greetings(n_row, n_col):
-    reaches, reach = [], 1
-    while reach < max(n_row, n_col) - 1:
+
+
+def greetings(n_row):
+    reaches, reach = [], REACH
+    while reach < n_row - 1:
         reaches.append(reach)
         reach *= 2
     return reaches
@@ -313,7 +327,7 @@
             pltpu.SemaphoreType.DMA((ITERS, 9)),
             pltpu.SemaphoreType.DMA((ITERS,)),
             pltpu.SemaphoreType.DMA((ITERS,)),
-            pltpu.SemaphoreType.REGULAR((max(1, len(greetings(n_row, n_col))),)),
+            pltpu.SemaphoreType.REGULAR((max(1, len(greetings(n_row))),)),
         ],
         compiler_params=pltpu.CompilerParams(
             collective_id=0, has_side_effects=True, vmem_limit_bytes=60 << 20),

time: 33.1 us -> 30.9 us (0.934)
  Pallas kernels: 32.3 us -> 30.1 us
    pallas_call x1, Pallas kernels: 31.7 us -> 29.5 us  [on_device(): pl.pallas_call(functools.partial(kernel, n_row, n_col), out_shape=(pltpu....]
where the time goes in v3:
time: 30.9 us; the launch traced here: 30.7 us
  Pallas kernels  30.1 us (97%)
  between operations  0.64 us (2%)
    pallas_call x1, Pallas kernels, on_device(): pl.pallas_call(functools.partial(kernel, n_row, n_col), out_shape=(pltpu....  29.5 us

profile of v3, /device:TPU:0, one launch (start us, length us, event | category | flops | bytes accessed | tf_op | source)
XLA Modules:
  0.0 30.7 jit_solution(13446119886013928404)
XLA Ops:
  0.6 29.5 %shard_map.68 = (f32[1,1,8,128]{3,2,1,0:T(8,128)S(1)}, f32[4,5]{1,0:T(4,128)S(1)}) custom-call(s32[1,1,4,8]{3,2,1,0:T(4,128)} %bitcast.2, s32[1,1,8]{2,1,0:T(1,128)} %live_ref.1, f32[1,1,8,128]{3,2,1,0:T(8,128)} %rhs_hbm.1, f32[1,1,8,128]{3,2,1,0:T(8,128)} %scale_hbm.1, bf16[1,1,8,4,128,128]{5,4,3,2,1,0:T(8,128)(2,1)} %vals_hbm.1), custom_call_target="tpu_custom_call" | custom-call | tf_op jit(solution)/shard_map/pallas_call | solution.py:306
  30.1 0.6 %shard_map.69 = (f32[1,1,8,128]{3,2,1,0:T(8,128)}, f32[4,5]{1,0:T(4,128)}) custom-call(f32[1,1,8,128]{3,2,1,0:T(8,128)S(1)} %get-tuple-element.6.field_ref, f32[4,5]{1,0:T(4,128)S(1)} %get-tuple-element.7.hess_ref), custom_call_target="tpu_custom_call" | custom-call | tf_op jit(solution)/shard_map/pallas_call | solution.py:337
